TPU v7x, 32 devices: a whole 2x2x4 slice. The times are simulated.
32 devices in a mesh: feat: 8 (over z, y), row: 2 (over x), col: 2 (over core).
Axes of the slice: x: 2, y: 2, z: 4, core: 2. Of those that a mesh axis runs over, the one named last changes fastest.
Arguments:
- local_x: float32 [4, 32, 256], P(('row', 'col'), 'feat'), may hold values from -4 to 4
- dual_var: float32 [4, 32, 256], P(('row', 'col'), 'feat'), may hold values from -2 to 2
- consensus_old: float32 [32, 256], P('feat'), may hold values from -4 to 4
- blocks_data: bfloat16 [4, 32, 512, 256], P(('row', 'col'), 'feat'), may hold values from -0.375 to 0.375
- row_index: int32 [4, 32, 512], P(('row', 'col'), 'feat'), may hold values from 0 to 16383, as said below
- labels: int32 [4, 16384], P(('row', 'col')), may hold values 0 or 1
Outputs:
- solved_x: float32 [4, 32, 256], P(('row', 'col'), 'feat')
- dual_new: float32 [4, 32, 256], P(('row', 'col'), 'feat')
- consensus: float32 [32, 256], P('feat')
- norms: float32 [2], replicated
Inputs may be any that keep to these rules, and one draw needn't show every extreme that they name: `row_index`: the 512 rows of one block are distinct samples of its shard; a sample may appear in no block or in several.
All inputs are finite; a program needn't handle non-finite values. No bound on the sum of `labels` on one device may be relied on, other than what follows from the above.
Results may differ from a plain program's by a relative error of at most 0.0019.
Values sent between devices are 32-bit elements; how exact they have to be, the bound alone decides.
A program may use at most 64 MiB of HBM per device.

v0:
```python
import jax
import jax.numpy as jnp
from jax import lax
from jax.sharding import PartitionSpec as P

NEWTON_STEPS = 2
CG_STEPS = 3


penalty = 1.0
damping = 0.5
threshold = 0.05


def shrink(values):
    return jnp.sign(values) * jnp.maximum(jnp.abs(values) - threshold, 0.0)


def conjugate_solve(hessian, gradient):
    delta = jnp.zeros_like(gradient)
    residual = gradient
    direction = gradient
    power = jnp.sum(residual * residual, axis=1)
    for cg_step in range(CG_STEPS):
        image = jnp.einsum("bkl,bl->bk", hessian, direction, precision=lax.Precision.HIGHEST)
        alpha = power / jnp.sum(direction * image, axis=1)
        delta = delta + alpha[:, None] * direction
        residual = residual - alpha[:, None] * image
        power_next = jnp.sum(residual * residual, axis=1)
        direction = residual + (power_next / power)[:, None] * direction
        power = power_next
    return delta


def local(local_x, dual_var, consensus_old, blocks_data, row_index, labels):
    iterate = local_x[0]
    dual_local = dual_var[0]
    block_rows = blocks_data[0]
    index_rows = row_index[0]
    targets = labels[0].astype(jnp.float32)
    samples = targets.shape[0]
    target = consensus_old - dual_local
    flat_index = index_rows.reshape(-1)
    identity = jnp.eye(iterate.shape[1], dtype=jnp.float32)
    for newton_step in range(NEWTON_STEPS):
        rounded = iterate.astype(jnp.bfloat16)
        partial_value = jnp.einsum(
            "brk,bk->br", block_rows, rounded, preferred_element_type=jnp.float32
        )
        local_margins = jax.ops.segment_sum(
            partial_value.reshape(-1), flat_index, num_segments=samples
        )
        margins = lax.psum(local_margins, "feat")
        prob = jax.nn.sigmoid(margins)
        misfit = prob - targets
        weights = prob * (1.0 - prob)
        misfit_rows = misfit[index_rows].astype(jnp.bfloat16)
        gradient = jnp.einsum(
            "brk,br->bk", block_rows, misfit_rows, preferred_element_type=jnp.float32
        )
        gradient = gradient + penalty * (iterate - target)
        weighted = (block_rows * weights[index_rows][:, :, None]).astype(jnp.bfloat16)
        hessian = (
            jnp.einsum("brk,brl->bkl", block_rows, weighted, preferred_element_type=jnp.float32)
            + penalty * identity
        )
        delta = conjugate_solve(hessian, gradient)
        iterate = iterate - damping * delta
    shards = lax.axis_size(("row", "col"))
    combined = iterate + dual_local
    totals = lax.psum(combined, ("row", "col"))
    consensus = shrink(totals / jnp.float32(shards))
    dual_next = dual_local + iterate - consensus
    primal_local = jnp.sum((iterate - consensus) ** 2)
    change_local = jnp.sum((consensus - consensus_old) ** 2)
    primal_total, change_total = lax.psum(
        (primal_local, change_local / jnp.float32(shards)), ("feat", "row", "col")
    )
    norms = jnp.stack(
        [jnp.sqrt(primal_total), penalty * jnp.sqrt(jnp.float32(shards) * change_total)]
    )
    return (iterate[None], dual_next[None], consensus, norms)


def solution(mesh):
    placed = (
        P(("row", "col"), "feat", None),
        P(("row", "col"), "feat", None),
        P("feat", None),
        P(("row", "col"), "feat", None, None),
        P(("row", "col"), "feat", None),
        P(("row", "col"), None),
    )
    return jax.shard_map(
        local,
        mesh=mesh,
        in_specs=placed,
        out_specs=(
            P(("row", "col"), "feat", None),
            P(("row", "col"), "feat", None),
            P("feat", None),
            P(),
        ),
        check_vma=False,
    )
```

profile of v0, /device:TPU:0, one launch (start us, length us, event | category | flops | bytes accessed | tf_op | source)
XLA Modules:
  0.0 292.5 jit_solution(3661908139111151564)
XLA Ops:
  7.2 0.7 fusion.62
  7.9 1.6 fusion.26
  9.6 11.8 %scatter_custom_fusion = f32[16384]{0:T(1024)} fusion(s32[2048]{0:T(1024)S(1)} %bitcast.146, f32[2048]{0:T(1024)S(1)} %bitcast.149, f32[]{:T(128)} %constant.9.clone.1), kind=kCustom, calls=%fused_computation.36 | custom fusion | flops 2048 | bytes 65540 | tf_op jit(solution)/shard_map/scatter-add | solution.py:50
  21.6 72.0 %all-reduce.4.cloned.1.call-done = f32[16384]{0:T(1024)} async-done(((f32[16384]{0:T(1024)}), f32[16384]{0:T(1024)}) %all-reduce.4.cloned.1.call-update) | async-done | bytes 65552 | tf_op jit(solution)/shard_map/psum | solution.py:53
  93.5 0.9 subtract_multiply_fusion.1
  94.4 11.8 %gather_fusion.1 = f32[2048]{0:T(1024)S(1)} fusion(f32[16384]{0:T(1024)S(1)} %subtract_multiply_fusion.1, s32[2048]{0:T(1024)S(1)} %broadcast_clamp_fusion), kind=kCustom, calls=%fused_computation.1 | custom fusion | bytes 24576 | tf_op jit(solution)/shard_map/gather | solution.py:62
  106.3 13.1 %gather_fusion = bf16[2048]{0:T(1024)(128)(2,1)S(1)} fusion(bf16[16384]{0:T(1024)(128)(2,1)S(1)} %fusion.35, s32[2048]{0:T(1024)S(1)} %broadcast_clamp_fusion), kind=kCustom, calls=%fused_computation | custom fusion | bytes 16384 | tf_op jit(solution)/shard_map/gather | solution.py:57
  119.7 0.9 fusion.9
  120.6 0.7 fusion.59
  121.7 0.7 fusion.57
  122.8 0.7 fusion.55
  124.1 11.8 %scatter_custom_fusion.1 = f32[16384]{0:T(1024)} fusion(s32[2048]{0:T(1024)S(1)} %bitcast.147, f32[2048]{0:T(1024)S(1)} %bitcast.148, f32[]{:T(128)} %constant.9.clone.1), kind=kCustom, calls=%fused_computation.34 | custom fusion | flops 2048 | bytes 65540 | tf_op jit(solution)/shard_map/scatter-add | solution.py:50
  135.9 69.3 %all-reduce.6.cloned.1.call-done = f32[16384]{0:T(1024)} async-done(((f32[16384]{0:T(1024)}), f32[16384]{0:T(1024)}) %all-reduce.6.cloned.1.call-update) | async-done | bytes 65552 | tf_op jit(solution)/shard_map/psum | solution.py:53
  205.3 0.9 fusion.36
  206.2 13.1 %gather_fusion.2 = bf16[2048]{0:T(1024)(128)(2,1)S(1)} fusion(bf16[16384]{0:T(1024)(128)(2,1)S(1)} %fusion.36, s32[2048]{0:T(1024)S(1)} %broadcast_clamp_fusion), kind=kCustom, calls=%fused_computation.2 | custom fusion | bytes 16384 | tf_op jit(solution)/shard_map/gather | solution.py:57
  219.3 11.8 %gather_fusion.3 = f32[2048]{0:T(1024)S(1)} fusion(f32[16384]{0:T(1024)S(1)} %subtract_multiply_fusion, s32[2048]{0:T(1024)S(1)} %broadcast_clamp_fusion), kind=kCustom, calls=%fused_computation.3 | custom fusion | bytes 24576 | tf_op jit(solution)/shard_map/gather | solution.py:62
  231.3 0.9 fusion.15
  232.3 0.7 fusion.52
  233.4 0.7 fusion.50
  234.5 0.7 fusion.48
  235.3 5.7 %psum.37 = f32[4,256]{1,0:T(4,128)S(1)} all-reduce(f32[4,256]{1,0:T(4,128)S(1)} %get-tuple-element.13), channel_id=1, replica_groups=mesh['feat'=8,'row'=2,'col'=2] {'row','col'}, use_global_device_ids=true, to_apply=%region_16.0 | all-reduce | flops 1024 | bytes 8192 | tf_op jit(solution)/shard_map/psum | solution.py:71
  241.0 0.7 multiply_reduce_fusion.1
  241.7 0.6 subtract_bitcast_fusion
  243.0 40.8 %all-reduce = (f32[]{:T(128)}, f32[]{:T(128)}) all-reduce(f32[]{:T(128)S(6)} %div.99, f32[]{:T(128)} %get-tuple-element.4), channel_id=1, replica_groups=mesh['feat'=8,'row'=2,'col'=2] {'feat','row','col'}, use_global_device_ids=true, to_apply=%region_20.0 | all-reduce | flops 2 | bytes 16 | tf_op jit(solution)/shard_map/psum | solution.py:76
  (72 shorter events, 3.9 us)
Async XLA Ops:
  7.2 2.4 copy-start.7
  7.2 14.3 %copy-start.3 = (s32[1,16384]{1,0:T(1,128)S(1)}, s32[1,16384]{1,0:T(1,128)}, u32[]{:S(2)}) copy-start(s32[1,16384]{1,0:T(1,128)} %param.11) | copy-start | bytes 196612
  7.2 86.4 %all-reduce.4.cloned.1.call-start = ((), (), s32[]{:S(2)}) async-start(), calls=%async_computation | async-start | bytes 131072 | tf_op jit(solution)/shard_map/psum | solution.py:53
  21.4 183.9 %all-reduce.6.cloned.1.call-start = ((), (), s32[]{:S(2)}) async-start(), calls=%async_computation.1 | async-start | bytes 131072 | tf_op jit(solution)/shard_map/psum | solution.py:53
  94.4 11.8 %copy-start.1 = (f32[16384]{0:T(1024)S(1)}, f32[16384]{0:T(1024)}, u32[]{:S(2)}) copy-start(f32[16384]{0:T(1024)} %all-reduce.4.cloned.1.call-done) | copy-start | bytes 196612
  106.3 13.1 %copy-start = (bf16[1,4,512,256]{3,2,1,0:T(8,128)(2,1)S(1)}, bf16[1,4,512,256]{3,2,1,0:T(8,128)(2,1)}, u32[]{:S(2)}) copy-start(bf16[1,4,512,256]{3,2,1,0:T(8,128)(2,1)} %param.9) | copy-start | bytes 3145732
  119.6 0.9 copy-start.4
  119.6 1.0 copy-start.5
  119.6 1.0 copy-start.6
  206.1 13.1 %copy-start.2 = (f32[16384]{0:T(1024)S(1)}, f32[16384]{0:T(1024)}, u32[]{:S(2)}) copy-start(f32[16384]{0:T(1024)} %all-reduce.6.cloned.1.call-done) | copy-start | bytes 196612
  235.3 50.3 %copy-start.9 = (f32[4,256]{1,0:T(4,128)}, f32[4,256]{1,0:T(4,128)S(1)}, u32[]{:S(2)}) copy-start(f32[4,256]{1,0:T(4,128)S(1)} %get-tuple-element.14) | copy-start | bytes 12292
  241.7 44.0 %copy-start.8 = (f32[4,256]{1,0:T(4,128)}, f32[4,256]{1,0:T(4,128)S(1)}, u32[]{:S(2)}) copy-start(f32[4,256]{1,0:T(4,128)S(1)} %get-tuple-element.12) | copy-start | bytes 12292
Sparse Core Ops, SparseCore 0:
  21.5 71.9 all-reduce.3
  136.0 69.1 all-reduce.5
where the time goes:
time: 293 us; the launch traced here: 292 us
  waiting for transfers between devices  141 us (48%)
  local copies, waits for them, and re-layouts  49.8 us (17%)
  blocking collectives  46.4 us (16%)
  other arithmetic  30.1 us (10%)
  between operations  16.4 us (6%)
  matrix products  8.28 us (3%)
    psum x2, waiting for transfers between devices, local(): margins = lax.psum(local_margins, 'feat')  141 us
    psum x1, blocking collectives, local(): lax.psum((primal_local, change_local / jnp.float32(shards)), ('feat', 'ro...  40.8 us
    gather x2, local copies, waits for them, and re-layouts, local(): misfit_rows = misfit[index_rows].astype(jnp.bfloat16)  26.2 us
    scatter-add x2, other arithmetic, local(): jax.ops.segment_sum(partial_value.reshape(-1), flat_index, num_segments=s...  23.7 us
    gather x4, local copies, waits for them, and re-layouts, local(): weights[index_rows][:, :, None]  23.6 us
  transfers between devices with their start and end apart: 2, of which 2 were waited for; matrix products, arithmetic and copies ran while one was open for 0% of the time, Pallas kernels for 0%

commit v1 on v0

v1 whole, which is shorter than its diff:
```python
import functools

import jax
import jax.numpy as jnp
from jax import lax
from jax.experimental import pallas as pl
from jax.experimental.pallas import tpu as pltpu
from jax.sharding import PartitionSpec as P

NEWTON_STEPS = 2
CG_STEPS = 3

penalty = 1.0
damping = 0.5
threshold = 0.05

MESH = pl.DeviceIdType.MESH
F32 = jnp.float32
BF16 = jnp.bfloat16
LANES = 128


def dot_nt(a, b):
    return lax.dot_general(a, b, (((1,), (1,)), ((), ())), preferred_element_type=F32)


def dot_nn(a, b):
    return lax.dot_general(a, b, (((1,), (0,)), ((), ())), preferred_element_type=F32)


def two_terms(value):
    high = value.astype(BF16).astype(F32)
    return high, value - high


def stacked(value):
    return jnp.concatenate(two_terms(value), axis=0).astype(BF16)


def kernel(
    n, rows, cols,
    lx, dual, cons, idx, lab, data_hbm,
    sx_out, dn_out, co_out, norm_out,
    data, p_all, idx_all, fin, nrm, oh_hi, oh_lo,
    data_sem, idx_ss, idx_rs, p_ss, p_rs, fin_ss, fin_rs, nrm_ss, nrm_rs,
):
    shards = rows * cols
    _, blocks, height, width = data_hbm.shape
    high_size = lab.shape[0]
    me = lax.axis_index("feat")
    shard = lax.axis_index("row") * cols + lax.axis_index("col")

    load = pltpu.make_async_copy(data_hbm.at[0], data, data_sem)
    load.start()

    barrier = pltpu.get_barrier_semaphore()

    def shard_id(other):
        return {"row": other // cols, "col": other % cols}

    @pl.loop(1, n)
    def _(k):
        pl.semaphore_signal(
            barrier, inc=1, device_id={"feat": (me + k) % n}, device_id_type=MESH)

    for j in range(1, shards):
        pl.semaphore_signal(
            barrier, inc=1, device_id=shard_id((shard + j) % shards), device_id_type=MESH)

    def feat_copy(src, dst, send, recv, target):
        return pltpu.make_async_remote_copy(
            src_ref=src, dst_ref=dst, send_sem=send, recv_sem=recv,
            device_id={"feat": target}, device_id_type=MESH)

    def sends(src, dst, send, recv):
        @pl.loop(1, n)
        def _(k):
            feat_copy(src, dst.at[me], send.at[k], recv.at[me], (me + k) % n).start()

    def wait_from(src, dst, send, recv, k):
        source = (me + n - k) % n
        feat_copy(src, dst.at[source], send.at[k], recv.at[source], (me + k) % n).wait_recv()
        return source

    def wait_sends(src, dst, send, recv):
        @pl.loop(1, n)
        def _(k):
            feat_copy(src, dst.at[me], send.at[k], recv.at[me], (me + k) % n).wait_send()

    def one_hot(index_row, size):
        lane = lax.broadcasted_iota(jnp.int32, (size, height), 0)
        return lane == index_row

    own = idx[0]
    labels_hl = lab[...].astype(F32).astype(BF16)
    targets = []
    for b in range(blocks):
        row = own[b:b + 1, :]
        high = one_hot(row // LANES, high_size).astype(F32)
        low = one_hot(row % LANES, LANES).astype(F32)
        oh_hi[b] = high.astype(BF16)
        oh_lo[b] = low.astype(BF16)
        picked = dot_nn(labels_hl, low.astype(BF16))
        targets.append(jnp.sum(picked * high, axis=0, keepdims=True))

    pl.semaphore_wait(barrier, n - 1 + shards - 1)
    sends(idx.at[0], idx_all, idx_ss, idx_rs)

    iterate = lx[0]
    dual_local = dual[0]
    target = cons[...] - dual_local
    load.wait()
    flat = data[...].reshape(blocks * height, width)
    block_of = lax.broadcasted_iota(jnp.int32, (blocks, height), 0)

    def place(pieces):
        return jnp.concatenate(
            [jnp.where(block_of == b, pieces[b], 0.0) for b in range(blocks)], axis=1)

    def scatter(index, values):
        total = jnp.zeros((LANES, 2 * high_size), F32)
        first, second = two_terms(values)
        for b in range(blocks):
            row = index[b:b + 1, :]
            mask = one_hot(row // LANES, high_size)
            low = one_hot(row % LANES, LANES).astype(F32).astype(BF16)
            spread = jnp.concatenate(
                [jnp.where(mask, first[b:b + 1, :], 0.0).astype(BF16),
                 jnp.where(mask, second[b:b + 1, :], 0.0).astype(BF16)], axis=0)
            total += dot_nt(low, spread)
        return total

    for step in range(NEWTON_STEPS):
        slots = p_all.at[step]
        products = dot_nt(iterate.astype(BF16), flat)
        partial_value = jnp.concatenate(
            [products[b:b + 1, b * height:(b + 1) * height] for b in range(blocks)], axis=0)
        slots[me] = partial_value
        sends(slots.at[me], slots, p_ss.at[step], p_rs.at[step])
        total = scatter(own, partial_value)

        def collect(k, total):
            if step == 0:
                wait_from(idx.at[0], idx_all, idx_ss, idx_rs, k)
            source = wait_from(slots.at[me], slots, p_ss.at[step], p_rs.at[step], k)
            return total + scatter(idx_all[source], slots[source])

        total = lax.fori_loop(1, n, collect, total)
        margins_t = total[:, :high_size] + total[:, high_size:]
        margins_two = stacked(margins_t)
        misfit, weights = [], []
        for b in range(blocks):
            picked = dot_nn(margins_two, oh_hi[b])
            both = picked[:LANES] + picked[LANES:]
            margin = jnp.sum(both * oh_lo[b].astype(F32), axis=0, keepdims=True)
            prob = 1.0 / (1.0 + jnp.exp(-margin))
            misfit.append(prob - targets[b])
            weights.append(prob * (1.0 - prob))
        weight_place = place(weights)
        gradient = dot_nn(place(misfit).astype(BF16), flat) + penalty * (iterate - target)

        delta = jnp.zeros_like(gradient)
        residual = gradient
        direction = gradient
        power = jnp.sum(residual * residual, axis=1, keepdims=True)
        for cg_step in range(CG_STEPS):
            product = dot_nt(stacked(direction), flat)
            scaled = (product[:blocks] + product[blocks:]) * weight_place
            image = dot_nn(stacked(scaled), flat)
            image = image[:blocks] + image[blocks:] + penalty * direction
            alpha = power / jnp.sum(direction * image, axis=1, keepdims=True)
            delta = delta + alpha * direction
            if cg_step < CG_STEPS - 1:
                residual = residual - alpha * image
                power_next = jnp.sum(residual * residual, axis=1, keepdims=True)
                direction = residual + (power_next / power) * direction
                power = power_next
        iterate = iterate - damping * delta

    fin[shard, 0] = iterate + dual_local
    fin[shard, 1] = iterate

    def fin_copy(j, slot):
        return pltpu.make_async_remote_copy(
            src_ref=fin.at[shard], dst_ref=fin.at[slot],
            send_sem=fin_ss.at[j], recv_sem=fin_rs.at[slot],
            device_id=shard_id((shard + j) % shards), device_id_type=MESH)

    for j in range(1, shards):
        fin_copy(j, shard).start()
    for j in range(1, shards):
        fin_copy(j, (shard + shards - j) % shards).wait_recv()
    totals = fin[0, 0]
    for s in range(1, shards):
        totals += fin[s, 0]
    averaged = totals / F32(shards)
    size = jnp.maximum(jnp.abs(averaged) - threshold, 0.0)
    consensus = jnp.where(averaged > 0.0, size, -size)
    change = (consensus - cons[...]) ** 2
    primal = (fin[0, 1] - consensus) ** 2
    for s in range(1, shards):
        primal += (fin[s, 1] - consensus) ** 2
    nrm[me] = jnp.concatenate(
        [jnp.sum(primal, axis=0, keepdims=True), jnp.sum(change, axis=0, keepdims=True)], axis=0)
    sends(nrm.at[me], nrm, nrm_ss, nrm_rs)
    sx_out[0] = iterate
    dn_out[0] = dual_local + iterate - consensus
    co_out[...] = consensus
    for j in range(1, shards):
        fin_copy(j, shard).wait_send()
    wait_sends(idx.at[0], idx_all, idx_ss, idx_rs)
    for step in range(NEWTON_STEPS):
        slots = p_all.at[step]
        wait_sends(slots.at[me], slots, p_ss.at[step], p_rs.at[step])

    @pl.loop(1, n)
    def _(k):
        wait_from(nrm.at[me], nrm, nrm_ss, nrm_rs, k)

    sums = jnp.sum(jnp.sum(nrm[...], axis=0), axis=1, keepdims=True)
    factor = lax.broadcasted_iota(jnp.int32, sums.shape, 0)
    scaled = jnp.where(factor == 0, sums, F32(shards) * sums)
    norms = jnp.sqrt(scaled) * jnp.where(factor == 0, 1.0, penalty)
    norm_out[0] = norms[0, 0]
    norm_out[1] = norms[1, 0]
    wait_sends(nrm.at[me], nrm, nrm_ss, nrm_rs)


def local(mesh, local_x, dual_var, consensus_old, blocks_data, row_index, labels):
    n, rows, cols = mesh.shape["feat"], mesh.shape["row"], mesh.shape["col"]
    shards = rows * cols
    _, blocks, height, width = blocks_data.shape
    samples = labels.shape[1]
    high_size = samples // LANES
    dma = pltpu.SemaphoreType.DMA
    vmem = pl.BlockSpec(memory_space=pltpu.VMEM)
    return pl.pallas_call(
        functools.partial(kernel, n, rows, cols),
        out_shape=(
            jax.ShapeDtypeStruct(local_x.shape, F32),
            jax.ShapeDtypeStruct(local_x.shape, F32),
            jax.ShapeDtypeStruct(consensus_old.shape, F32),
            jax.ShapeDtypeStruct((2,), F32),
        ),
        in_specs=[vmem] * 5 + [pl.BlockSpec(memory_space=pl.ANY)],
        out_specs=(vmem, vmem, vmem, pl.BlockSpec(memory_space=pltpu.SMEM)),
        scratch_shapes=[
            pltpu.VMEM((blocks, height, width), BF16),
            pltpu.VMEM((NEWTON_STEPS, n, blocks, height), F32),
            pltpu.VMEM((n, blocks, height), jnp.int32),
            pltpu.VMEM((shards, 2, blocks, width), F32),
            pltpu.VMEM((n, 2, width), F32),
            pltpu.VMEM((blocks, high_size, height), BF16),
            pltpu.VMEM((blocks, LANES, height), BF16),
            dma,
            dma((n,)), dma((n,)),
            dma((NEWTON_STEPS, n)), dma((NEWTON_STEPS, n)),
            dma((shards,)), dma((shards,)),
            dma((n,)), dma((n,)),
        ],
        compiler_params=pltpu.CompilerParams(
            collective_id=0, has_side_effects=True, vmem_limit_bytes=56 * 1024 * 1024),
        name="admm",
    )(local_x, dual_var, consensus_old, row_index, labels.reshape(high_size, LANES), blocks_data)


def solution(mesh):
    placed = (
        P(("row", "col"), "feat", None),
        P(("row", "col"), "feat", None),
        P("feat", None),
        P(("row", "col"), "feat", None, None),
        P(("row", "col"), "feat", None),
        P(("row", "col"), None),
    )
    return jax.shard_map(
        functools.partial(local, mesh),
        mesh=mesh,
        in_specs=placed,
        out_specs=(
            P(("row", "col"), "feat", None),
            P(("row", "col"), "feat", None),
            P("feat", None),
            P(),
        ),
        check_vma=False,
    )
```

time: 293 us -> 39.2 us (0.13)
  waiting for transfers between devices: 141 us -> 0 us
  local copies, waits for them, and re-layouts: 49.8 us -> 3.14 us
  blocking collectives: 46.4 us -> 0 us
  Pallas kernels: 0 us -> 35.2 us
  other arithmetic: 30.1 us -> 0 us
  between operations: 16.4 us -> 0.65 us
  matrix products: 8.28 us -> 0 us
    psum x2 -> x0, waiting for transfers between devices: 141 us -> none  [local(): margins = lax.psum(local_margins, 'feat')]
    gather x6 -> x0, local copies, waits for them, and re-layouts: 49.7 us -> none  [the longest x2 26.2 us: local(): misfit_rows = misfit[index_rows].astype(jnp.bfloat16)]
    psum x2 -> x0, blocking collectives: 46.4 us -> none  [the longest x1 40.8 us: local(): lax.psum((primal_local, change_local / jnp.float32(shards)), ('feat', 'ro...]
    pallas_call x0 -> x1, Pallas kernels: none -> 35.2 us  [local(): pl.pallas_call(functools.partial(kernel, n, rows, cols), out_shape=(jax.S...]
    scatter-add x2 -> x0, other arithmetic: 23.7 us -> none  [local(): jax.ops.segment_sum(partial_value.reshape(-1), flat_index, num_segments=s...]
    dot_general x12 -> x0, matrix products: 8.28 us -> none  [the longest x6 3.96 us: conjugate_solve(): jnp.einsum('bkl,bl->bk', hessian, direction, precision=lax.Precision.HIGH...]
    unnamed x24 -> x12, local copies, waits for them, and re-layouts: 0.07 us -> 3.14 us
  transfers between devices with their start and end apart: 2 -> 0, of which waited for: 2 -> 0; matrix products, arithmetic and copies ran while one was open for 0% -> 0% of each run, Pallas kernels for 0% -> 0%
where the time goes in v1:
time: 39.2 us; the launch traced here: 39 us
  Pallas kernels  35.2 us (90%)
  local copies, waits for them, and re-layouts  3.14 us (8%)
  between operations  0.65 us (2%)
    pallas_call x1, Pallas kernels, local(): pl.pallas_call(functools.partial(kernel, n, rows, cols), out_shape=(jax.S...  35.2 us
    unnamed x12, local copies, waits for them, and re-layouts  3.14 us

profile of v1, /device:TPU:0, one launch (start us, length us, event | category | flops | bytes accessed | tf_op | source)
XLA Modules:
  0.0 39.0 jit_solution(11305205999731024802)
XLA Ops:
  0.6 35.2 %admm.1 = (f32[1,4,256]{2,1,0:T(4,128)}, f32[1,4,256]{2,1,0:T(4,128)}, f32[4,256]{1,0:T(4,128)}, f32[2]{0:T(128)}) custom-call(f32[1,4,256]{2,1,0:T(4,128)} %lx.1, f32[1,4,256]{2,1,0:T(4,128)} %dual.1, f32[4,256]{1,0:T(4,128)} %cons.1, s32[1,4,512]{2,1,0:T(4,128)} %idx.1, s32[128,128]{1,0:T(8,128)} %bitcast.1, bf16[1,4,512,256]{3,2,1,0:T(8,128)(2,1)} %data_hbm.1), custom_call_target="tpu_custom_call" | custom-call | tf_op jit(solution)/shard_map/admm/pallas_call | solution.py:237
  35.8 0.0 copy-start.2
  35.8 0.7 %copy-done.2 = f32[1,4,256]{2,1,0:T(4,128)S(1)} copy-done((f32[1,4,256]{2,1,0:T(4,128)S(1)}, f32[1,4,256]{2,1,0:T(4,128)}, u32[]{:S(2)}) %copy-start.2) | copy-done | bytes 4120
  36.5 0.0 copy-start.1
  36.5 0.6 %copy.14 = f32[1,4,256]{2,1,0:T(4,128)} copy(f32[1,4,256]{2,1,0:T(4,128)S(1)} %copy-done.2) | data formatting | bytes 8192
  37.1 0.1 copy-done.1
  37.2 0.0 copy-start
  37.2 0.6 %copy.15 = f32[1,4,256]{2,1,0:T(4,128)} copy(f32[1,4,256]{2,1,0:T(4,128)S(1)} %copy-done.1) | data formatting | bytes 8192
  37.8 0.1 copy-done
  37.8 0.0 copy-start.3
  37.8 0.6 %copy.16 = f32[4,256]{1,0:T(4,128)} copy(f32[4,256]{1,0:T(4,128)S(1)} %copy-done) | data formatting | bytes 8192
  38.4 0.0 copy-done.3
  38.4 0.5 %copy.17 = f32[2]{0:T(128)} copy(f32[2]{0:T(128)S(1)} %copy-done.3) | data formatting | bytes 16
Async XLA Ops:
  35.8 0.7 %copy-start.2 = (f32[1,4,256]{2,1,0:T(4,128)S(1)}, f32[1,4,256]{2,1,0:T(4,128)}, u32[]{:S(2)}) copy-start(f32[1,4,256]{2,1,0:T(4,128)} %get-tuple-element.8) | copy-start | bytes 12292
  36.5 0.7 %copy-start.1 = (f32[1,4,256]{2,1,0:T(4,128)S(1)}, f32[1,4,256]{2,1,0:T(4,128)}, u32[]{:S(2)}) copy-start(f32[1,4,256]{2,1,0:T(4,128)} %get-tuple-element.9) | copy-start | bytes 12292
  37.2 0.7 %copy-start = (f32[4,256]{1,0:T(4,128)S(1)}, f32[4,256]{1,0:T(4,128)}, u32[]{:S(2)}) copy-start(f32[4,256]{1,0:T(4,128)} %get-tuple-element.10) | copy-start | bytes 12292
  37.8 0.6 %copy-start.3 = (f32[2]{0:T(128)S(1)}, f32[2]{0:T(128)}, u32[]{:S(2)}) copy-start(f32[2]{0:T(128)} %get-tuple-element.11) | copy-start | bytes 28

commit v2 on v1

v2 whole, which is shorter than its diff:
```python
import functools

import jax
import jax.numpy as jnp
from jax import lax
from jax.experimental import pallas as pl
from jax.experimental.pallas import tpu as pltpu
from jax.sharding import PartitionSpec as P

NEWTON_STEPS = 2
CG_STEPS = 3

penalty = 1.0
damping = 0.5
threshold = 0.05

MESH = pl.DeviceIdType.MESH
F32 = jnp.float32
BF16 = jnp.bfloat16
LANE_BITS = 7
LANES = 1 << LANE_BITS


def dot_nt(a, b):
    return lax.dot_general(a, b, (((1,), (1,)), ((), ())), preferred_element_type=F32)


def dot_nn(a, b):
    return lax.dot_general(a, b, (((1,), (0,)), ((), ())), preferred_element_type=F32)


def two_terms(value):
    high = value.astype(BF16).astype(F32)
    return high, value - high


def kernel(
    n, rows, cols,
    lx_hbm, dual_hbm, cons_hbm, idx_hbm, lab_hbm, data_hbm,
    packed_out,
    lx, dual, cons, lab, data, data_t, hess, p_all, idx_all, fin, nrm, oh_hi, oh_lo,
    in_sem, idx_ss, idx_rs, p_ss, p_rs, fin_ss, fin_rs, nrm_ss, nrm_rs,
):
    shards = rows * cols
    blocks, height, width = data.shape
    high_size = lab.shape[0]
    me = lax.axis_index("feat")
    shard = lax.axis_index("row") * cols + lax.axis_index("col")

    loads = [
        pltpu.make_async_copy(source, place, in_sem.at[i])
        for i, (source, place) in enumerate([
            (idx_hbm.at[0], idx_all.at[me]),
            (data_hbm.at[0], data),
            (lab_hbm, lab),
            (lx_hbm.at[0], lx),
            (dual_hbm.at[0], dual),
            (cons_hbm, cons),
        ])
    ]
    for load in loads:
        load.start()

    barrier = pltpu.get_barrier_semaphore()

    def shard_id(other):
        return {"row": other // cols, "col": other % cols}

    @pl.loop(1, n)
    def _(k):
        pl.semaphore_signal(
            barrier, inc=1, device_id={"feat": (me + k) % n}, device_id_type=MESH)

    for j in range(1, shards):
        pl.semaphore_signal(
            barrier, inc=1, device_id=shard_id((shard + j) % shards), device_id_type=MESH)

    def feat_copy(src, dst, send, recv, target):
        return pltpu.make_async_remote_copy(
            src_ref=src, dst_ref=dst, send_sem=send, recv_sem=recv,
            device_id={"feat": target}, device_id_type=MESH)

    def sends(dst, send, recv):
        @pl.loop(1, n)
        def _(k):
            feat_copy(dst.at[me], dst.at[me], send.at[k], recv.at[me], (me + k) % n).start()

    def wait_from(dst, send, recv, k):
        source = (me + n - k) % n
        feat_copy(
            dst.at[source], dst.at[source], send.at[k], recv.at[source], (me + k) % n).wait_recv()
        return source

    def wait_sends(dst, send, recv):
        @pl.loop(1, n)
        def _(k):
            feat_copy(
                dst.at[me], dst.at[me], send.at[k], recv.at[me], (me + k) % n).wait_send()

    def hits(index_row, size):
        level = lax.broadcasted_iota(jnp.int32, (size, height), 0).astype(F32).astype(BF16)
        return level == index_row.astype(F32).astype(BF16)

    def high_hits(index_row):
        return hits(index_row >> LANE_BITS, high_size)

    def low_hits(index_row):
        return hits(index_row & (LANES - 1), LANES)

    one, zero = jnp.ones((), BF16), jnp.zeros((), BF16)

    for load in loads:
        load.wait()
    iterate = lx[...]
    dual_local = dual[...]
    target = cons[...] - dual_local

    own = idx_all[me]
    labels_hl = lab[...].astype(F32).astype(BF16)
    targets = []
    for b in range(blocks):
        row = own[b:b + 1, :]
        low = jnp.where(low_hits(row), one, zero)
        high = jnp.where(high_hits(row), one, zero)
        oh_hi[b] = high
        oh_lo[b] = low
        picked = dot_nn(labels_hl, low)
        targets.append(jnp.sum(picked * high.astype(F32), axis=0, keepdims=True))
        data_t[b] = data[b].T

    def products(iterate):
        rounded = iterate.astype(BF16)
        return jnp.concatenate(
            [dot_nn(rounded, data_t[b])[b:b + 1] for b in range(blocks)], axis=0)

    partial_value = products(iterate)
    p_all[0, me] = partial_value

    pl.semaphore_wait(barrier, n - 1 + shards - 1)
    sends(idx_all, idx_ss, idx_rs)

    def scatter(index, values):
        total = jnp.zeros((2 * high_size, LANES), F32)
        first, second = two_terms(values)
        first, second = first.astype(BF16), second.astype(BF16)
        for b in range(blocks):
            row = index[b:b + 1, :]
            mask = high_hits(row)
            low = jnp.where(low_hits(row), one, zero)
            spread = jnp.concatenate(
                [jnp.where(mask, first[b:b + 1, :], zero),
                 jnp.where(mask, second[b:b + 1, :], zero)], axis=0)
            total += dot_nt(spread, low)
        return total

    for step in range(NEWTON_STEPS):
        slots = p_all.at[step]
        if step > 0:
            partial_value = products(iterate)
            slots[me] = partial_value
        sends(slots, p_ss.at[step], p_rs.at[step])
        total = scatter(own, partial_value)

        def collect(k, total):
            if step == 0:
                wait_from(idx_all, idx_ss, idx_rs, k)
            source = wait_from(slots, p_ss.at[step], p_rs.at[step], k)
            return total + scatter(idx_all[source], slots[source])

        total = lax.fori_loop(1, n, collect, total)
        margins = total[:high_size] + total[high_size:]
        margins_two = jnp.concatenate(two_terms(margins), axis=0).astype(BF16)
        gradient = []
        for b in range(blocks):
            picked = dot_nn(margins_two, oh_lo[b])
            both = picked[:high_size] + picked[high_size:]
            margin = jnp.sum(both * oh_hi[b].astype(F32), axis=0, keepdims=True)
            prob = 1.0 / (1.0 + jnp.exp(-margin))
            weights = prob * (1.0 - prob)
            misfit = jnp.broadcast_to(prob - targets[b], (16, height))
            left = jnp.concatenate(
                [(data_t[b].astype(F32) * weights).astype(BF16), misfit.astype(BF16)], axis=0)
            made = dot_nn(left, data[b])
            hess[b] = made[:width]
            gradient.append(made[width:width + 1])
        gradient = jnp.concatenate(gradient, axis=0) + penalty * (iterate - target)

        delta = jnp.zeros_like(gradient)
        residual = gradient
        direction = gradient
        power = jnp.sum(residual * residual, axis=1, keepdims=True)
        for cg_step in range(CG_STEPS):
            turned = direction.T
            image = jnp.concatenate(
                [jnp.sum(hess[b] * turned[:, b:b + 1], axis=0, keepdims=True)
                 for b in range(blocks)], axis=0) + penalty * direction
            alpha = power / jnp.sum(direction * image, axis=1, keepdims=True)
            delta = delta + alpha * direction
            if cg_step < CG_STEPS - 1:
                residual = residual - alpha * image
                power_next = jnp.sum(residual * residual, axis=1, keepdims=True)
                direction = residual + (power_next / power) * direction
                power = power_next
        iterate = iterate - damping * delta

    fin[shard, 0] = iterate + dual_local
    fin[shard, 1] = iterate

    def fin_copy(j, slot):
        return pltpu.make_async_remote_copy(
            src_ref=fin.at[shard], dst_ref=fin.at[slot],
            send_sem=fin_ss.at[j], recv_sem=fin_rs.at[slot],
            device_id=shard_id((shard + j) % shards), device_id_type=MESH)

    for j in range(1, shards):
        fin_copy(j, shard).start()
    for j in range(1, shards):
        fin_copy(j, (shard + shards - j) % shards).wait_recv()
    totals = fin[0, 0]
    for s in range(1, shards):
        totals += fin[s, 0]
    averaged = totals / F32(shards)
    size = jnp.maximum(jnp.abs(averaged) - threshold, 0.0)
    consensus = jnp.where(averaged > 0.0, size, -size)
    change = (consensus - cons[...]) ** 2
    primal = (fin[0, 1] - consensus) ** 2
    for s in range(1, shards):
        primal += (fin[s, 1] - consensus) ** 2
    nrm[me] = jnp.concatenate(
        [jnp.sum(primal, axis=0, keepdims=True), jnp.sum(change, axis=0, keepdims=True)], axis=0)
    sends(nrm, nrm_ss, nrm_rs)
    packed_out[0] = iterate
    packed_out[1] = dual_local + iterate - consensus
    packed_out[2] = consensus
    for j in range(1, shards):
        fin_copy(j, shard).wait_send()
    wait_sends(idx_all, idx_ss, idx_rs)
    for step in range(NEWTON_STEPS):
        wait_sends(p_all.at[step], p_ss.at[step], p_rs.at[step])

    @pl.loop(1, n)
    def _(k):
        wait_from(nrm, nrm_ss, nrm_rs, k)

    sums = jnp.sum(jnp.sum(nrm[...], axis=0), axis=1, keepdims=True)
    factor = lax.broadcasted_iota(jnp.int32, sums.shape, 0)
    scaled = jnp.where(factor == 0, sums, F32(shards) * sums)
    norms = jnp.sqrt(scaled) * jnp.where(factor == 0, 1.0, penalty)
    packed_out[3, :2] = jnp.broadcast_to(norms, (2, width))
    wait_sends(nrm, nrm_ss, nrm_rs)


def unpack(packed, sx_out, dn_out, co_out, norm_out):
    sx_out[0] = packed[0]
    dn_out[0] = packed[1]
    co_out[...] = packed[2]
    norm_out[0] = packed[3, 0, 0]
    norm_out[1] = packed[3, 1, 0]


def local(mesh, local_x, dual_var, consensus_old, blocks_data, row_index, labels):
    n, rows, cols = mesh.shape["feat"], mesh.shape["row"], mesh.shape["col"]
    shards = rows * cols
    _, blocks, height, width = blocks_data.shape
    samples = labels.shape[1]
    high_size = samples // LANES
    dma = pltpu.SemaphoreType.DMA
    vmem = pl.BlockSpec(memory_space=pltpu.VMEM)
    packed = pl.pallas_call(
        functools.partial(kernel, n, rows, cols),
        out_shape=jax.ShapeDtypeStruct((4, max(blocks, 2), width), F32),
        in_specs=[pl.BlockSpec(memory_space=pl.ANY)] * 6,
        out_specs=vmem,
        scratch_shapes=[
            pltpu.VMEM((blocks, width), F32),
            pltpu.VMEM((blocks, width), F32),
            pltpu.VMEM((blocks, width), F32),
            pltpu.VMEM((high_size, LANES), jnp.int32),
            pltpu.VMEM((blocks, height, width), BF16),
            pltpu.VMEM((blocks, width, height), BF16),
            pltpu.VMEM((blocks, width, width), F32),
            pltpu.VMEM((NEWTON_STEPS, n, blocks, height), F32),
            pltpu.VMEM((n, blocks, height), jnp.int32),
            pltpu.VMEM((shards, 2, blocks, width), F32),
            pltpu.VMEM((n, 2, width), F32),
            pltpu.VMEM((blocks, high_size, height), BF16),
            pltpu.VMEM((blocks, LANES, height), BF16),
            dma((6,)),
            dma((n,)), dma((n,)),
            dma((NEWTON_STEPS, n)), dma((NEWTON_STEPS, n)),
            dma((shards,)), dma((shards,)),
            dma((n,)), dma((n,)),
        ],
        compiler_params=pltpu.CompilerParams(
            collective_id=0, has_side_effects=True, vmem_limit_bytes=56 * 1024 * 1024),
        name="admm",
    )(local_x, dual_var, consensus_old, row_index, labels.reshape(high_size, LANES), blocks_data)
    return pl.pallas_call(
        unpack,
        out_shape=(
            jax.ShapeDtypeStruct(local_x.shape, F32),
            jax.ShapeDtypeStruct(local_x.shape, F32),
            jax.ShapeDtypeStruct(consensus_old.shape, F32),
            jax.ShapeDtypeStruct((2,), F32),
        ),
        in_specs=[vmem],
        out_specs=(vmem, vmem, vmem, pl.BlockSpec(memory_space=pltpu.SMEM)),
        name="unpack",
    )(packed)


def solution(mesh):
    placed = (
        P(("row", "col"), "feat", None),
        P(("row", "col"), "feat", None),
        P("feat", None),
        P(("row", "col"), "feat", None, None),
        P(("row", "col"), "feat", None),
        P(("row", "col"), None),
    )
    return jax.shard_map(
        functools.partial(local, mesh),
        mesh=mesh,
        in_specs=placed,
        out_specs=(
            P(("row", "col"), "feat", None),
            P(("row", "col"), "feat", None),
            P("feat", None),
            P(),
        ),
        check_vma=False,
    )
```

time: 39.2 us -> 34.8 us (0.89)
  local copies, waits for them, and re-layouts: 3.14 us -> 0 us
  Pallas kernels: 35.2 us -> 33.9 us
    unnamed x12 -> x0, local copies, waits for them, and re-layouts: 3.14 us -> none
    pallas_call x1 -> x2, Pallas kernels: 35.2 us -> 33.9 us  [the longest x1 32.5 us: local(): pl.pallas_call(functools.partial(kernel, n, rows, cols), out_shape=jax.Sh...]
where the time goes in v2:
time: 34.8 us; the launch traced here: 34.5 us
  Pallas kernels  33.9 us (97%)
  between operations  0.64 us (2%)
    pallas_call x1, Pallas kernels, local(): pl.pallas_call(functools.partial(kernel, n, rows, cols), out_shape=jax.Sh...  32.5 us
    pallas_call x1, Pallas kernels, local(): pl.pallas_call(unpack, out_shape=(jax.ShapeDtypeStruct(local_x.shape, F32...  1.33 us

profile of v2, /device:TPU:0, one launch (start us, length us, event | category | flops | bytes accessed | tf_op | source)
XLA Modules:
  0.0 34.5 jit_solution(18027823388032918206)
XLA Ops:
  0.6 32.5 %admm.1.packed = f32[4,4,256]{2,1,0:T(4,128)} custom-call(f32[1,4,256]{2,1,0:T(4,128)} %lx_hbm.1, f32[1,4,256]{2,1,0:T(4,128)} %dual_hbm.1, f32[4,256]{1,0:T(4,128)} %cons_hbm.1, s32[1,4,512]{2,1,0:T(4,128)} %idx_hbm.1, s32[128,128]{1,0:T(8,128)} %bitcast.1, bf16[1,4,512,256]{3,2,1,0:T(8,128)(2,1)} %data_hbm.1), custom_call_target="tpu_custom_call" | custom-call | tf_op jit(solution)/shard_map/admm/pallas_call | solution.py:269
  33.2 1.3 %unpack.1 = (f32[1,4,256]{2,1,0:T(4,128)}, f32[1,4,256]{2,1,0:T(4,128)}, f32[4,256]{1,0:T(4,128)}, f32[2]{0:T(128)}) custom-call(f32[4,4,256]{2,1,0:T(4,128)} %admm.1.packed), custom_call_target="tpu_custom_call" | custom-call | tf_op jit(solution)/shard_map/unpack/pallas_call | solution.py:298

commit v3 on v2

--- a/solution.py
+++ b/solution.py
@@ -109,7 +109,10 @@
 
     one, zero = jnp.ones((), BF16), jnp.zeros((), BF16)
 
-    for load in loads:
+    loads[0].wait()
+    pl.semaphore_wait(barrier, n - 1 + shards - 1)
+    sends(idx_all, idx_ss, idx_rs)
+    for load in loads[1:]:
         load.wait()
     iterate = lx[...]
     dual_local = dual[...]
@@ -132,12 +135,6 @@
         rounded = iterate.astype(BF16)
         return jnp.concatenate(
             [dot_nn(rounded, data_t[b])[b:b + 1] for b in range(blocks)], axis=0)
-
-    partial_value = products(iterate)
-    p_all[0, me] = partial_value
-
-    pl.semaphore_wait(barrier, n - 1 + shards - 1)
-    sends(idx_all, idx_ss, idx_rs)
 
     def scatter(index, values):
         total = jnp.zeros((2 * high_size, LANES), F32)
@@ -153,21 +150,24 @@
             total += dot_nt(spread, low)
         return total
 
-    for step in range(NEWTON_STEPS):
-        slots = p_all.at[step]
-        if step > 0:
-            partial_value = products(iterate)
-            slots[me] = partial_value
-        sends(slots, p_ss.at[step], p_rs.at[step])
-        total = scatter(own, partial_value)
+    def newton_step(step, iterate):
+        slots, slot_ss, slot_rs = p_all.at[step], p_ss.at[step], p_rs.at[step]
+        slots[me] = products(iterate)
+        sends(slots, slot_ss, slot_rs)
 
         def collect(k, total):
-            if step == 0:
+            @pl.when((step == 0) & (k > 0))
+            def _():
                 wait_from(idx_all, idx_ss, idx_rs, k)
-            source = wait_from(slots, p_ss.at[step], p_rs.at[step], k)
+
+            @pl.when(k > 0)
+            def _():
+                wait_from(slots, slot_ss, slot_rs, k)
+
+            source = (me + n - k) % n
             return total + scatter(idx_all[source], slots[source])
 
-        total = lax.fori_loop(1, n, collect, total)
+        total = lax.fori_loop(0, n, collect, jnp.zeros((2 * high_size, LANES), F32))
         margins = total[:high_size] + total[high_size:]
         margins_two = jnp.concatenate(two_terms(margins), axis=0).astype(BF16)
         gradient = []
@@ -185,23 +185,25 @@
             gradient.append(made[width:width + 1])
         gradient = jnp.concatenate(gradient, axis=0) + penalty * (iterate - target)
 
-        delta = jnp.zeros_like(gradient)
-        residual = gradient
-        direction = gradient
-        power = jnp.sum(residual * residual, axis=1, keepdims=True)
-        for cg_step in range(CG_STEPS):
+        def cg_step(_, state):
+            delta, residual, direction, power = state
             turned = direction.T
             image = jnp.concatenate(
                 [jnp.sum(hess[b] * turned[:, b:b + 1], axis=0, keepdims=True)
                  for b in range(blocks)], axis=0) + penalty * direction
             alpha = power / jnp.sum(direction * image, axis=1, keepdims=True)
             delta = delta + alpha * direction
-            if cg_step < CG_STEPS - 1:
-                residual = residual - alpha * image
-                power_next = jnp.sum(residual * residual, axis=1, keepdims=True)
-                direction = residual + (power_next / power) * direction
-                power = power_next
-        iterate = iterate - damping * delta
+            residual = residual - alpha * image
+            power_next = jnp.sum(residual * residual, axis=1, keepdims=True)
+            direction = residual + (power_next / power) * direction
+            return delta, residual, direction, power_next
+
+        power = jnp.sum(gradient * gradient, axis=1, keepdims=True)
+        delta = lax.fori_loop(
+            0, CG_STEPS, cg_step, (jnp.zeros_like(gradient), gradient, gradient, power))[0]
+        return iterate - damping * delta
+
+    iterate = lax.fori_loop(0, NEWTON_STEPS, newton_step, iterate)
 
     fin[shard, 0] = iterate + dual_local
     fin[shard, 1] = iterate

time: 34.8 us -> 34.7 us (level)
  no operation moved by 1% of the time
where the time goes in v3:
time: 34.7 us; the launch traced here: 34.4 us
  Pallas kernels  33.8 us (97%)
  between operations  0.64 us (2%)
    pallas_call x1, Pallas kernels, local(): pl.pallas_call(functools.partial(kernel, n, rows, cols), out_shape=jax.Sh...  32.4 us
    pallas_call x1, Pallas kernels, local(): pl.pallas_call(unpack, out_shape=(jax.ShapeDtypeStruct(local_x.shape, F32...  1.33 us

profile of v3, /device:TPU:0, one launch (start us, length us, event | category | flops | bytes accessed | tf_op | source)
XLA Modules:
  0.0 34.4 jit_solution(1637318766029848827)
XLA Ops:
  0.6 32.4 %admm.1.packed = f32[4,4,256]{2,1,0:T(4,128)} custom-call(f32[1,4,256]{2,1,0:T(4,128)} %lx_hbm.1, f32[1,4,256]{2,1,0:T(4,128)} %dual_hbm.1, f32[4,256]{1,0:T(4,128)} %cons_hbm.1, s32[1,4,512]{2,1,0:T(4,128)} %idx_hbm.1, s32[128,128]{1,0:T(8,128)} %bitcast.1, bf16[1,4,512,256]{3,2,1,0:T(8,128)(2,1)} %data_hbm.1), custom_call_target="tpu_custom_call" | custom-call | tf_op jit(solution)/shard_map/admm/pallas_call | solution.py:271
  33.1 1.3 %unpack.1 = (f32[1,4,256]{2,1,0:T(4,128)}, f32[1,4,256]{2,1,0:T(4,128)}, f32[4,256]{1,0:T(4,128)}, f32[2]{0:T(128)}) custom-call(f32[4,4,256]{2,1,0:T(4,128)} %admm.1.packed), custom_call_target="tpu_custom_call" | custom-call | tf_op jit(solution)/shard_map/unpack/pallas_call | solution.py:300
